TPU v7x, 32 devices: a whole 2x2x4 slice. The times are simulated.
32 devices in a mesh: tm: 16 (over z, y, core), chan: 2 (over x).
Axes of the slice: x: 2, y: 2, z: 4, core: 2. Of those that a mesh axis runs over, the one named last changes fastest.
Arguments:
- signal: bfloat16 [32768, 512], P('tm', 'chan'), may hold values from -72 to 72
- tapers: bfloat16 [8, 4096], replicated, may hold values from -0.09375 to 0.09375
- eigenvalues: float32 [8], replicated, may hold values from 0.05 to 1
Outputs:
- relative_psd: float32 [2048, 512], P('tm', 'chan')
All inputs are finite; a program needn't handle non-finite values.
Results may differ from a plain program's by a relative error of at most 0.0026.
The roundings to bfloat16 on the way count: a program that leaves them out, or rounds other values in their place, can miss the bound.
Values may be sent and summed in bfloat16 or wider, within the bound.
No kernel may reach another device: no remote copies, remote signals or barrier semaphores. Data moves between devices by JAX's collectives and lax.ppermute only.
A program may use at most 64 MiB of HBM per device.

v0:
```python
import math
import jax
import jax.numpy as jnp
from jax import lax
from jax.sharding import PartitionSpec as P

P_SIZE = 32
Q = 128
EPSILON = 1e-06


def dft_tables(outer_size, inner_size):
    inner = jnp.arange(inner_size, dtype=jnp.int32)
    outer = jnp.arange(outer_size, dtype=jnp.int32)
    halves = jnp.arange(outer_size // 2, dtype=jnp.int32)
    angle_first = (inner[:, None] * inner[None, :] % inner_size).astype(jnp.float32) * (
        2.0 * math.pi / inner_size
    )
    first_table = jnp.concatenate([jnp.cos(angle_first), -jnp.sin(angle_first)], axis=0).astype(
        jnp.bfloat16
    )
    angle_twist = (inner[:, None] * outer[None, :] % (outer_size * inner_size)).astype(
        jnp.float32
    ) * (2.0 * math.pi / (outer_size * inner_size))
    twist_cos = jnp.cos(angle_twist)[:, :, None, None]
    twist_sin = jnp.sin(angle_twist)[:, :, None, None]
    angle_last = (outer[:, None] * halves[None, :] % outer_size).astype(jnp.float32) * (
        2.0 * math.pi / outer_size
    )
    last_cos = jnp.cos(angle_last).astype(jnp.bfloat16)
    last_sin = jnp.sin(angle_last).astype(jnp.bfloat16)
    return (first_table, twist_cos, twist_sin, last_cos, last_sin)


def taper_power(tapered, tables):
    first_table, twist_cos, twist_sin, last_cos, last_sin = tables
    inner_size = tapered.shape[0]
    first = jnp.einsum("jn,npsc->jpsc", first_table, tapered, preferred_element_type=jnp.float32)
    first_real = first[:inner_size]
    first_imaginary = first[inner_size:]
    twist_real = (first_real * twist_cos + first_imaginary * twist_sin).astype(jnp.bfloat16)
    twist_imaginary = (first_imaginary * twist_cos - first_real * twist_sin).astype(jnp.bfloat16)
    last_real = jnp.einsum(
        "pa,kpsc->aksc", last_cos, twist_real, preferred_element_type=jnp.float32
    ) + jnp.einsum("pa,kpsc->aksc", last_sin, twist_imaginary, preferred_element_type=jnp.float32)
    last_imaginary = jnp.einsum(
        "pa,kpsc->aksc", last_cos, twist_imaginary, preferred_element_type=jnp.float32
    ) - jnp.einsum("pa,kpsc->aksc", last_sin, twist_real, preferred_element_type=jnp.float32)
    return last_real * last_real + last_imaginary * last_imaginary


def local(signal, tapers, eigenvalues):
    row_count, chan_count = signal.shape
    outer_size = P_SIZE
    inner_size = Q
    stride = tapers.shape[1] // 2
    half_inner = inner_size // 2
    tm_size = lax.axis_size("tm")
    samples = signal.astype(jnp.float32)
    common = lax.psum(jnp.sum(samples, axis=1), "chan") / (chan_count * lax.axis_size("chan"))
    referenced = (samples - common[:, None]).astype(jnp.bfloat16)
    all_rows = row_count * tm_size
    segments = all_rows // stride - 1
    tables = dft_tables(outer_size, inner_size)
    weights = eigenvalues / jnp.sum(eigenvalues)
    taper_grid = tapers.reshape(tapers.shape[0], inner_size, outer_size, 1, 1)
    columns = lax.all_to_all(referenced, "tm", split_axis=1, concat_axis=0, tiled=True)
    narrow = columns.shape[1]
    widened = columns.astype(jnp.float32)
    centre = jnp.sum(widened, axis=0) / all_rows
    variance = jnp.sum((widened - centre) ** 2, axis=0) / all_rows
    halves = columns.reshape(all_rows // stride, half_inner, outer_size, narrow)
    halves = jnp.transpose(halves, (1, 2, 0, 3))
    windows = jnp.concatenate([halves[:, :, :-1], halves[:, :, 1:]], axis=0)

    def add_column_taper(taper, accumulated):
        taper_row = lax.dynamic_index_in_dim(taper_grid, taper, 0, keepdims=False).astype(
            jnp.float32
        )
        tapered = ((windows.astype(jnp.float32) - centre) * taper_row).astype(jnp.bfloat16)
        power = taper_power(tapered, tables)
        return accumulated + weights[taper] * jnp.sum(power, axis=2).reshape(stride, narrow)

    total = lax.fori_loop(
        0, tapers.shape[0], add_column_taper, jnp.zeros((stride, narrow), jnp.float32)
    )
    density = total / segments / (variance + EPSILON)
    return lax.all_to_all(density, "tm", split_axis=0, concat_axis=1, tiled=True)


def solution(mesh):
    return jax.shard_map(
        local,
        mesh=mesh,
        in_specs=(P("tm", "chan"), P(), P()),
        out_specs=P("tm", "chan"),
        check_vma=False,
    )
```

profile of v0, /device:TPU:0, one launch (start us, length us, event | category | flops | bytes accessed | tf_op | source)
XLA Modules:
  0.0 131.2 jit_solution(6070422819959520975)
XLA Ops:
  0.0 1.5 %copy.30 = bf16[2048,256]{0,1:T(8,128)(2,1)S(1)} copy(bf16[2048,256]{1,0:T(8,128)(2,1)} %param.5) | data formatting | bytes 2097152 | tf_op args[0]
  1.7 5.9 %psum.7 = f32[2048]{0:T(1024)S(1)} all-reduce(f32[2048]{0:T(1024)S(1)} %convert_reduce_fusion.1), channel_id=1, replica_groups=mesh['tm'=16,'chan'=2] {'chan'}, use_global_device_ids=true, to_apply=%region_1.0 | all-reduce | flops 2048 | bytes 16384 | tf_op jit(solution)/shard_map/psum | solution.py:60
  7.6 1.2 fusion.55
  8.8 6.5 %all-to-all-start = ((bf16[2048,16,16]{0,2,1:T(8,128)(2,1)}), bf16[2048,16,16]{0,2,1:T(8,128)(2,1)S(1)}, u32[]{:S(2)}, u32[]{:S(2)}) async-start(bf16[2048,16,16]{0,2,1:T(8,128)(2,1)} %bitcast), calls=%async_computation | async-start | bytes 2097152 | tf_op jit(solution)/shard_map/all_to_all | solution.py:67
  17.4 20.9 %all-to-all-done = bf16[2048,16,16]{0,2,1:T(8,128)(2,1)S(1)} async-done(((bf16[2048,16,16]{0,2,1:T(8,128)(2,1)}), bf16[2048,16,16]{0,2,1:T(8,128)(2,1)S(1)}, u32[]{:S(2)}, u32[]{:S(2)}) %all-to-all-start) | async-done | bytes 1048608 | tf_op jit(solution)/shard_map/all_to_all | solution.py:67
  39.2 4.4 %reshape.113 = bf16[16,64,32,16]{2,1,3,0:T(8,128)(2,1)} reshape(bf16[16,2048,16]{1,2,0:T(8,128)(2,1)S(1)} %bitcast.71) | data formatting | bytes 2097152 | tf_op jit(solution)/shard_map/reshape | solution.py:72
  43.6 7.0 %fusion.64 = (bf16[64,32,15,16]{1,0,3,2:T(8,128)(2,1)}, bf16[64,32,15,16]{1,0,3,2:T(8,128)(2,1)}) fusion(bf16[64,32,16,16]{1,0,3,2:T(8,128)(2,1)} %bitcast.70), kind=kLoop, calls=%fused_computation.89 | loop fusion | bytes 3932160 | tf_op jit(solution)/shard_map/slice | solution.py:74
  50.6 5.8 %copy.31 = bf16[64,32,15,16]{0,3,2,1:T(8,128)(2,1)} copy(bf16[64,32,15,16]{1,0,3,2:T(8,128)(2,1)} %get-tuple-element.308) | data formatting | bytes 1966080 | tf_op jit(solution)/shard_map/slice | solution.py:74
  56.5 5.8 %copy.32 = bf16[64,32,15,16]{0,3,2,1:T(8,128)(2,1)} copy(bf16[64,32,15,16]{1,0,3,2:T(8,128)(2,1)} %get-tuple-element.309) | data formatting | bytes 1966080 | tf_op jit(solution)/shard_map/slice | solution.py:74
  62.2 3.2 %pad_maximum_fusion = bf16[128,32,15,16]{0,3,2,1:T(8,128)(2,1)S(1)} fusion(bf16[64,32,15,16]{0,3,2,1:T(8,128)(2,1)} %copy.32, bf16[64,32,15,16]{0,3,2,1:T(8,128)(2,1)} %copy.31), kind=kLoop, calls=%fused_computation.70 | loop fusion | flops 3932160 | bytes 3932160 | tf_op jit(solution)/shard_map/concatenate | solution.py:74
  65.4 50.4 %while.15 = (s32[]{:T(128)}, f32[2048,16]{0,1:T(8,128)S(1)}, f32[8]{0:T(128)S(1)}, bf16[128,32,15,16]{0,3,2,1:T(8,128)(2,1)S(1)}, f32[16]{0:T(128)S(1)}, /*index...) while((s32[]{:T(128)}, f32[2048,16]{0,1:T(8,128)S(1)}, ...), condition=%wide.region_6.7_spmd.clone.clone, body=%wide.region_4.6_spmd.clone.clone.sunk | while | flops 644048896 | bytes 42246336 | solution.py:84
  66.2 1.2 convolution_bitcast_fusion.2
  67.4 1.1 add_convert_fusion.2
  72.5 1.2 convolution_bitcast_fusion.2
  73.7 1.1 add_convert_fusion.2
  78.8 1.2 convolution_bitcast_fusion.2
  80.0 1.1 add_convert_fusion.2
  85.1 1.2 convolution_bitcast_fusion.2
  91.4 1.2 convolution_bitcast_fusion.2
  97.7 1.2 convolution_bitcast_fusion.2
  98.9 1.1 add_convert_fusion.2
  104.0 1.2 convolution_bitcast_fusion.2
  110.3 1.2 convolution_bitcast_fusion.2
  115.9 14.5 %all_to_all.35 = f32[16,128,16]{1,2,0:T(8,128)S(1)} all-to-all(f32[16,128,16]{1,2,0:T(8,128)S(1)} %copy_bitcast_fusion), channel_id=1, replica_groups=mesh['tm'=16,'chan'=2] {'tm'}, dimensions={0} | all-to-all | bytes 262144 | tf_op jit(solution)/shard_map/all_to_all | solution.py:88
  (95 shorter events, 39.6 us)
Async XLA Ops:
  7.6 7.7 %copy-start = (bf16[8,4096]{1,0:T(8,128)(2,1)S(1)}, bf16[8,4096]{1,0:T(8,128)(2,1)}, u32[]{:S(2)}) copy-start(bf16[8,4096]{1,0:T(8,128)(2,1)} %param.6) | copy-start | bytes 196612
  7.6 8.1 %copy-start.1 = (f32[8]{0:T(128)S(1)}, f32[8]{0:T(128)}, u32[]{:S(2)}) copy-start(f32[8]{0:T(128)} %param.7) | copy-start | bytes 100
  8.8 29.4 %all-to-all-start = ((bf16[2048,16,16]{0,2,1:T(8,128)(2,1)}), bf16[2048,16,16]{0,2,1:T(8,128)(2,1)S(1)}, u32[]{:S(2)}, u32[]{:S(2)}) async-start(bf16[2048,16,16]{0,2,1:T(8,128)(2,1)} %bitcast), calls=%async_computation | async-start | bytes 2097152 | tf_op jit(solution)/shard_map/all_to_all | solution.py:67
where the time goes:
time: 132 us; the launch traced here: 131 us
  local copies, waits for them, and re-layouts  30.9 us (23%)
  matrix products  28.8 us (22%)
  other arithmetic  23.2 us (18%)
  waiting for transfers between devices  20.9 us (16%)
  blocking collectives  20.4 us (15%)
  starting transfers between devices  6.47 us (5%)
    all_to_all x1, waiting for transfers between devices, local(): lax.all_to_all(referenced, 'tm', split_axis=1, concat_axis=0, tiled=True)  20.9 us
    slice x3, local copies, waits for them, and re-layouts, local(): windows = jnp.concatenate([halves[:, :, :-1], halves[:, :, 1:]], axis=0)  18.6 us
    all_to_all x1, blocking collectives, local(): lax.all_to_all(density, 'tm', split_axis=0, concat_axis=1, tiled=True)  14.5 us
    dot_general x8, matrix products, taper_power(): jnp.einsum('jn,npsc->jpsc', first_table, tapered, preferred_element_type=...  9.85 us
    convert_element_type x8, other arithmetic, taper_power(): (first_real * twist_cos + first_imaginary * twist_sin).astype(jnp.bfloat16)  8.88 us
    dot_general x8, matrix products, taper_power(): jnp.einsum('pa,kpsc->aksc', last_sin, twist_real, preferred_element_type=...  7.2 us
    all_to_all x1, starting transfers between devices, local(): lax.all_to_all(referenced, 'tm', split_axis=1, concat_axis=0, tiled=True)  6.47 us
    psum x1, blocking collectives, local(): lax.psum(jnp.sum(samples, axis=1), 'chan')  5.94 us
  transfers between devices with their start and end apart: 1, of which 1 were waited for; matrix products, arithmetic and copies ran while one was open for 2% of the time, Pallas kernels for 0%

commit v1 on v0

--- a/solution.py
+++ b/solution.py
@@ -64,7 +64,9 @@
     tables = dft_tables(outer_size, inner_size)
     weights = eigenvalues / jnp.sum(eigenvalues)
     taper_grid = tapers.reshape(tapers.shape[0], inner_size, outer_size, 1, 1)
-    columns = lax.all_to_all(referenced, "tm", split_axis=1, concat_axis=0, tiled=True)
+    shards = jnp.split(referenced, lax.axis_size("tm"), axis=1)
+    incoming = lax.all_to_all(jnp.stack(shards), "tm", 0, 0)
+    columns = jnp.concatenate(incoming, axis=0)
     narrow = columns.shape[1]
     widened = columns.astype(jnp.float32)
     centre = jnp.sum(widened, axis=0) / all_rows

time: 132 us -> 141 us (1.068)
  local copies, waits for them, and re-layouts: 30.9 us -> 40.9 us
    unnamed x6 -> x21, local copies, waits for them, and re-layouts: 1.62 us -> 11 us
    another operation x0 -> x2, local copies, waits for them, and re-layouts: none -> 5.09 us  [the longest x1 4.45 us: local(): halves = columns.reshape(all_rows // stride, half_inner, outer_size, narrow)]
    reshape x1 -> x0, local copies, waits for them, and re-layouts: 4.45 us -> none  [local(): halves = columns.reshape(all_rows // stride, half_inner, outer_size, narrow)]
  transfers between devices with their start and end apart: 1 -> 1, of which waited for: 1 -> 1; matrix products, arithmetic and copies ran while one was open for 2% -> 1% of each run, Pallas kernels for 0% -> 0%
where the time goes in v1:
time: 141 us
  local copies, waits for them, and re-layouts  40.9 us (29%)
  matrix products  28.7 us (20%)
  other arithmetic  22.9 us (16%)
  waiting for transfers between devices  20.9 us (15%)
  blocking collectives  20.4 us (14%)
  starting transfers between devices  6.47 us (5%)
    all_to_all x1, waiting for transfers between devices, local(): incoming = lax.all_to_all(jnp.stack(shards), 'tm', 0, 0)  20.9 us
    slice x3, local copies, waits for them, and re-layouts, local(): windows = jnp.concatenate([halves[:, :, :-1], halves[:, :, 1:]], axis=0)  18.6 us
    all_to_all x1, blocking collectives, local(): lax.all_to_all(density, 'tm', split_axis=0, concat_axis=1, tiled=True)  14.5 us
    unnamed x21, local copies, waits for them, and re-layouts  11 us
    dot_general x8, matrix products, taper_power(): jnp.einsum('jn,npsc->jpsc', first_table, tapered, preferred_element_type=...  9.84 us
    convert_element_type x8, other arithmetic, taper_power(): (first_real * twist_cos + first_imaginary * twist_sin).astype(jnp.bfloat16)  9.58 us
    dot_general x8, matrix products, taper_power(): jnp.einsum('pa,kpsc->aksc', last_sin, twist_real, preferred_element_type=...  7.2 us
    all_to_all x1, starting transfers between devices, local(): incoming = lax.all_to_all(jnp.stack(shards), 'tm', 0, 0)  6.47 us
  transfers between devices with their start and end apart: 1, of which 1 were waited for; matrix products, arithmetic and copies ran while one was open for 1% of the time, Pallas kernels for 0%

profile of v1, /device:TPU:0, one launch (start us, length us, event | category | flops | bytes accessed | tf_op | source)
XLA Modules:
  0.0 141.0 jit_solution(3581902538525283963)
XLA Ops:
  0.0 1.5 %copy.30 = bf16[2048,256]{0,1:T(8,128)(2,1)S(1)} copy(bf16[2048,256]{1,0:T(8,128)(2,1)} %param.5) | data formatting | bytes 2097152 | tf_op args[0]
  1.7 5.9 %psum.7 = f32[2048]{0:T(1024)S(1)} all-reduce(f32[2048]{0:T(1024)S(1)} %convert_reduce_fusion.1), channel_id=1, replica_groups=mesh['tm'=16,'chan'=2] {'chan'}, use_global_device_ids=true, to_apply=%region_1.0 | all-reduce | flops 2048 | bytes 16384 | tf_op jit(solution)/shard_map/psum | solution.py:60
  17.8 6.5 %all-to-all-start = ((bf16[16,2048,16]{1,2,0:T(8,128)(2,1)}), bf16[16,2048,16]{1,2,0:T(8,128)(2,1)S(1)}, u32[]{:S(2)}, u32[]{:S(2)}) async-start(bf16[16,2048,16]{1,2,0:T(8,128)(2,1)} %fusion.61), calls=%async_computation | async-start | bytes 2097152 | tf_op jit(solution)/shard_map/all_to_all | solution.py:68
  26.4 20.9 %all-to-all-done = bf16[16,2048,16]{1,2,0:T(8,128)(2,1)S(1)} async-done(((bf16[16,2048,16]{1,2,0:T(8,128)(2,1)}), bf16[16,2048,16]{1,2,0:T(8,128)(2,1)S(1)}, u32[]{:S(2)}, u32[]{:S(2)}) %all-to-all-start) | async-done | bytes 1048608 | tf_op jit(solution)/shard_map/all_to_all | solution.py:68
  48.2 4.4 %reshape_reshape.3 = bf16[16,64,32,16]{2,1,3,0:T(8,128)(2,1)} reshape(bf16[16,2048,16]{1,2,0:T(8,128)(2,1)S(1)} %all-to-all-done) | data formatting | bytes 2097152 | tf_op jit(solution)/shard_map/reshape;reshape | solution.py:74
  52.6 7.0 %fusion.80 = (bf16[64,32,15,16]{1,0,3,2:T(8,128)(2,1)}, bf16[64,32,15,16]{1,0,3,2:T(8,128)(2,1)}) fusion(bf16[64,32,16,16]{1,0,3,2:T(8,128)(2,1)} %bitcast.130), kind=kLoop, calls=%fused_computation.121 | loop fusion | bytes 3932160 | tf_op jit(solution)/shard_map/slice | solution.py:76
  59.6 5.8 %copy.31 = bf16[64,32,15,16]{0,3,2,1:T(8,128)(2,1)} copy(bf16[64,32,15,16]{1,0,3,2:T(8,128)(2,1)} %get-tuple-element.308) | data formatting | bytes 1966080 | tf_op jit(solution)/shard_map/slice | solution.py:76
  65.4 5.8 %copy.32 = bf16[64,32,15,16]{0,3,2,1:T(8,128)(2,1)} copy(bf16[64,32,15,16]{1,0,3,2:T(8,128)(2,1)} %get-tuple-element.309) | data formatting | bytes 1966080 | tf_op jit(solution)/shard_map/slice | solution.py:76
  71.2 3.2 %pad_maximum_fusion = bf16[128,32,15,16]{0,3,2,1:T(8,128)(2,1)S(1)} fusion(bf16[64,32,15,16]{0,3,2,1:T(8,128)(2,1)} %copy.32, bf16[64,32,15,16]{0,3,2,1:T(8,128)(2,1)} %copy.31), kind=kLoop, calls=%fused_computation.70 | loop fusion | flops 3932160 | bytes 3932160 | tf_op jit(solution)/shard_map/concatenate | solution.py:76
  74.4 51.2 %while.15 = (s32[]{:T(128)}, f32[2048,16]{0,1:T(8,128)S(1)}, f32[8]{0:T(128)S(1)}, bf16[128,32,15,16]{0,3,2,1:T(8,128)(2,1)S(1)}, f32[16]{0:T(128)S(1)}, /*index...) while((s32[]{:T(128)}, f32[2048,16]{0,1:T(8,128)S(1)}, ...), condition=%wide.region_6.7_spmd.clone.clone, body=%wide.region_4.6_spmd.clone.clone.sunk | while | flops 644048896 | bytes 42246328 | solution.py:86
  74.5 1.2 convolution_bitcast_fusion.2
  80.9 1.2 convolution_bitcast_fusion.2
  87.3 1.2 convolution_bitcast_fusion.2
  88.6 1.2 add_convert_fusion.2
  93.7 1.2 convolution_bitcast_fusion.2
  95.0 1.2 add_convert_fusion.2
  100.1 1.2 convolution_bitcast_fusion.2
  101.4 1.2 add_convert_fusion.2
  106.5 1.2 convolution_bitcast_fusion.2
  107.8 1.2 add_convert_fusion.2
  112.9 1.2 convolution_bitcast_fusion.2
  114.2 1.2 add_convert_fusion.2
  119.2 1.2 convolution_bitcast_fusion.2
  125.7 14.5 %all_to_all.24 = f32[16,128,16]{1,2,0:T(8,128)S(1)} all-to-all(f32[16,128,16]{1,2,0:T(8,128)S(1)} %copy_bitcast_fusion), channel_id=1, replica_groups=mesh['tm'=16,'chan'=2] {'tm'}, dimensions={0} | all-to-all | bytes 262144 | tf_op jit(solution)/shard_map/all_to_all | solution.py:90
  (111 shorter events, 49.0 us)
Async XLA Ops:
  9.1 15.2 %copy-start = (bf16[8,4096]{1,0:T(8,128)(2,1)S(1)}, bf16[8,4096]{1,0:T(8,128)(2,1)}, u32[]{:S(2)}) copy-start(bf16[8,4096]{1,0:T(8,128)(2,1)} %param.6) | copy-start | bytes 196612
  12.2 12.4 %copy-start.1 = (f32[8]{0:T(128)S(1)}, f32[8]{0:T(128)}, u32[]{:S(2)}) copy-start(f32[8]{0:T(128)} %param.7) | copy-start | bytes 100
  17.8 29.4 %all-to-all-start = ((bf16[16,2048,16]{1,2,0:T(8,128)(2,1)}), bf16[16,2048,16]{1,2,0:T(8,128)(2,1)S(1)}, u32[]{:S(2)}, u32[]{:S(2)}) async-start(bf16[16,2048,16]{1,2,0:T(8,128)(2,1)} %fusion.61), calls=%async_computation | async-start | bytes 2097152 | tf_op jit(solution)/shard_map/all_to_all | solution.py:68
